TPU v7x, 32 devices: a whole 2x2x4 slice. The times are simulated.
32 devices in a mesh: seq: 16 (over z, x, core), ch: 2 (over y).
Axes of the slice: x: 2, y: 2, z: 4, core: 2. Of those that a mesh axis runs over, the one named last changes fastest.
Arguments:
- out_grad: bfloat16 [2048, 4096], P('seq', 'ch'), may hold values from -6 to 6
- out_weight: bfloat16 [4096, 4096], P(('seq', 'ch')), may hold values from -0.09375 to 0.09375
- outer_gate: bfloat16 [2048, 4096], P('seq', 'ch'), may hold values from -6 to 6
- long_out: bfloat16 [2048, 4096], P('seq', 'ch'), may hold values from -6 to 6
- inner_gate: bfloat16 [2048, 4096], P('seq', 'ch'), may hold values from -6 to 6
- conv_input: bfloat16 [2048, 4096], P('seq', 'ch'), may hold values from -6 to 6
- short_out: bfloat16 [2048, 4096], P('seq', 'ch'), may hold values from -6 to 6
- medium_out: bfloat16 [2048, 4096], P('seq', 'ch'), may hold values from -6 to 6
- long_filter: bfloat16 [2048, 4096], P('seq', 'ch'), may hold values from -6 to 6
- taps_short: bfloat16 [7, 4096], P(None, 'ch'), may hold values from -2 to 2
- taps_medium: bfloat16 [128, 4096], P(None, 'ch'), may hold values from -0.5 to 0.5
Outputs:
- grad_outer: bfloat16 [2048, 4096], P('seq', 'ch')
- grad_inner: bfloat16 [2048, 4096], P('seq', 'ch')
- grad_input: bfloat16 [2048, 4096], P('seq', 'ch')
- grad_filter: float32 [2048, 4096], P('seq', 'ch')
- grad_short: float32 [7, 4096], P(None, 'ch')
- grad_medium: float32 [128, 4096], P(None, 'ch')
All inputs are finite; a program needn't handle non-finite values.
Results may differ from a plain program's by a relative error of at most 0.0065.
Values may be sent and summed in bfloat16 or wider, within the bound.
No kernel may reach another device: no remote copies, remote signals or barrier semaphores. Data moves between devices by JAX's collectives and lax.ppermute only.
A program may use at most 128 MiB of HBM per device.

v0:
```python
import math
import jax
import jax.numpy as jnp
from jax import lax
from jax.sharding import PartitionSpec as P

SHORT = 7
MEDIUM = 128
ACCURATE = lax.Precision.HIGH


def from_behind(value, axis, steps):
    count = lax.axis_size(axis)
    leading, last = (max(0, -steps), min(count, count - steps))
    return lax.ppermute(value, axis, [(source, source + steps) for source in range(leading, last)])


def rotation(numer, denom):
    angles = 2.0 * math.pi / denom * numer.astype(jnp.float32)
    return (jnp.cos(angles), jnp.sin(angles))


def dft_table(length, orient):
    indices = lax.iota(jnp.int32, length)
    cosine, sine_part = rotation(indices[:, None] * indices[None, :] % length, length)
    return (cosine, orient * sine_part)


def apply_table(table, real_part, imag_part, pattern):

    def multiply(left, right):
        return jnp.einsum(pattern, left, right, precision=ACCURATE)

    if imag_part is None:
        return (multiply(table[0], real_part), multiply(table[1], real_part))
    return (
        multiply(table[0], real_part) - multiply(table[1], imag_part),
        multiply(table[0], imag_part) + multiply(table[1], real_part),
    )


def real_table(table, real_part, imag_part, pattern):
    return jnp.einsum(pattern, table[0], real_part, precision=ACCURATE) - jnp.einsum(
        pattern, table[1], imag_part, precision=ACCURATE
    )


def twist(real_part, imag_part, cosine, sine_part):
    return (real_part * cosine - imag_part * sine_part, real_part * sine_part + imag_part * cosine)


def outer_forward(signal, time_pos, row_pos, freq_pos, total):
    table = dft_table(signal.shape[0], -1.0)
    cosine, sine_part = rotation(time_pos, 2 * total)
    shift_real, shift_imag = rotation(row_pos * freq_pos % total, total)
    outputs = []
    for parity in range(2):
        if parity == 0:
            real_part, imag_part = apply_table(table, signal, None, "ca,am->cm")
        else:
            real_part, imag_part = apply_table(
                table, signal * cosine, -signal * sine_part, "ca,am->cm"
            )
        outputs += list(twist(real_part, imag_part, shift_real, -shift_imag))
    return outputs


def inner_forward(parts):
    table = dft_table(parts[0].shape[0], -1.0)
    outputs = []
    for place in range(0, len(parts), 2):
        outputs += list(apply_table(table, parts[place], parts[place + 1], "br,rn->bn"))
    return outputs


def inner_inverse(parts, narrow, total):
    table = dft_table(parts[0].shape[0], 1.0)
    row_pos = lax.iota(jnp.int32, parts[0].shape[0])[:, None]
    freq_pos = lax.iota(jnp.int32, parts[0].shape[1])[None, :] // narrow
    shift_real, shift_imag = rotation(row_pos * freq_pos % total, total)
    outputs = []
    for place in range(0, len(parts), 2):
        real_part, imag_part = apply_table(table, parts[place], parts[place + 1], "rb,bn->rn")
        outputs += list(twist(real_part, imag_part, shift_real, shift_imag))
    return outputs


def outer_inverse(parts, time_pos, total):
    table = dft_table(parts[0].shape[0], 1.0)
    cosine, sine_part = rotation(time_pos, 2 * total)
    outputs = []
    for place in range(0, len(parts), 4):
        high_real, high_imag = apply_table(table, parts[place + 2], parts[place + 3], "ac,cm->am")
        high_real, high_imag = twist(high_real, high_imag, cosine, sine_part)
        outputs.append(real_table(table, parts[place], parts[place + 1], "ac,cm->am") + high_real)
    return outputs


def conj_times(left_real, left_imag, right_real, right_imag):
    return (
        left_real * right_real + left_imag * right_imag,
        left_real * right_imag - left_imag * right_real,
    )


def spectral_terms(spectra):
    first, second = ([], [])
    for parity in range(2):
        grad_real, grad_imag = (spectra[4 + 2 * parity], spectra[5 + 2 * parity])
        point_real, point_imag = conj_times(
            spectra[8 + 2 * parity], spectra[9 + 2 * parity], grad_real, grad_imag
        )
        filt_real, filt_imag = conj_times(
            spectra[2 * parity], spectra[2 * parity + 1], grad_real, grad_imag
        )
        first += [point_real, point_imag]
        second += [filt_real, filt_imag]
    return first + second


def depthwise(signal, kernel):
    channels = signal.shape[1]
    result = lax.conv_general_dilated(
        signal.astype(jnp.float32)[None],
        kernel.astype(jnp.float32)[:, None, :],
        (1,),
        "VALID",
        dimension_numbers=("NWC", "WIO", "NWC"),
        feature_group_count=channels,
        precision=lax.Precision.HIGHEST,
    )
    return result[0]


def adjoint_taps(extended, taps):
    return depthwise(extended, taps)


def tap_products(grads, extended):
    return depthwise(extended, grads)[::-1]


def per_device(
    out_grad,
    out_weight,
    outer_gate,
    long_out,
    inner_gate,
    conv_input,
    short_out,
    medium_out,
    long_filter,
    taps_short,
    taps_medium,
):
    height = out_grad.shape[0]
    channels = outer_gate.shape[1]
    devices = lax.axis_size("seq")
    total = height * devices
    earlier_short, earlier_input = from_behind(
        (short_out[height - (MEDIUM - 1) :], conv_input[height - (SHORT - 1) :]), "seq", 1
    )
    features = lax.all_gather(out_grad, "ch", axis=1, tiled=True)
    aligned = lax.all_to_all(out_weight, "ch", split_axis=1, concat_axis=0, tiled=True)
    hidden = jnp.dot(
        features,
        lax.all_gather(aligned, "seq", axis=0, tiled=True),
        preferred_element_type=jnp.float32,
    )
    grad_outer = (hidden * long_out.astype(jnp.float32)).astype(jnp.bfloat16)
    long_grad = (hidden * outer_gate.astype(jnp.float32)).astype(jnp.bfloat16)
    product = (inner_gate.astype(jnp.float32) * medium_out.astype(jnp.float32)).astype(jnp.bfloat16)
    narrow = channels // devices
    lane_span = height * narrow

    def to_blocks(signal):
        return (
            signal.reshape(height, devices, narrow).transpose(1, 0, 2).reshape(devices, lane_span)
        )

    def to_inner(signal):
        return (
            signal.reshape(devices, height, narrow)
            .transpose(1, 0, 2)
            .reshape(height, devices * narrow)
        )

    arrived = (
        lax.all_to_all(to_blocks(product), "seq", split_axis=0, concat_axis=0, tiled=True),
        lax.all_to_all(to_blocks(long_grad), "seq", split_axis=0, concat_axis=0, tiled=True),
        lax.all_to_all(to_blocks(long_filter), "seq", split_axis=0, concat_axis=0, tiled=True),
    )
    row_pos = lax.iota(jnp.int32, lane_span)[None, :] // narrow
    source = lax.iota(jnp.int32, devices)[:, None]
    time_pos = source * height + row_pos
    spread = []
    for signal in arrived:
        spread += outer_forward(signal.astype(jnp.float32), time_pos, row_pos, source, total)
    spectra = inner_forward([to_inner(piece) for piece in spread])
    terms = inner_inverse(spectral_terms(spectra), narrow, total)
    results = outer_inverse([to_blocks(piece) for piece in terms], time_pos, total)
    result = lax.all_to_all(jnp.stack(results), "seq", split_axis=1, concat_axis=1, tiled=True)
    result = (
        result.reshape(2, devices, height, narrow)
        .transpose(0, 2, 1, 3)
        .reshape(2, height, channels)
    )
    scale = total ** (-0.5) / (2.0 * total)
    point_grad = result[0] * scale
    grad_filter = result[1] * scale
    medium_grad = (point_grad * inner_gate.astype(jnp.float32)).astype(jnp.bfloat16)
    grad_inner = (point_grad * medium_out.astype(jnp.float32)).astype(jnp.bfloat16)
    later_medium = from_behind(medium_grad[: MEDIUM - 1], "seq", -1)
    short_grad = adjoint_taps(jnp.concatenate([medium_grad, later_medium]), taps_medium).astype(
        jnp.bfloat16
    )
    later_short = from_behind(short_grad[: SHORT - 1], "seq", -1)
    grad_input = adjoint_taps(jnp.concatenate([short_grad, later_short]), taps_short).astype(
        jnp.bfloat16
    )
    partial_medium = tap_products(medium_grad, jnp.concatenate([earlier_short, short_out]))
    partial_short = tap_products(short_grad, jnp.concatenate([earlier_input, conv_input]))
    sum_medium, sum_short = lax.psum((partial_medium, partial_short), "seq")
    factor = total ** (-0.5)
    return (
        grad_outer,
        grad_inner,
        grad_input,
        grad_filter,
        sum_short * factor,
        sum_medium * factor,
    )


def solution(mesh):
    return jax.shard_map(
        per_device,
        mesh=mesh,
        in_specs=(
            P("seq", "ch"),
            P(("seq", "ch"), None),
            P("seq", "ch"),
            P("seq", "ch"),
            P("seq", "ch"),
            P("seq", "ch"),
            P("seq", "ch"),
            P("seq", "ch"),
            P("seq", "ch"),
            P(None, "ch"),
            P(None, "ch"),
        ),
        out_specs=(
            P("seq", "ch"),
            P("seq", "ch"),
            P("seq", "ch"),
            P("seq", "ch"),
            P(None, "ch"),
            P(None, "ch"),
        ),
        check_vma=False,
    )
```

profile of v0, /device:TPU:0, one launch (start us, length us, event | category | flops | bytes accessed | tf_op | source)
XLA Modules:
  0.0 585.1 jit_solution(104122376312642344)
XLA Ops:
  9.6 24.2 %all_to_all.63 = bf16[128,2,2048]{0,2,1:T(8,128)(2,1)S(1)} all-to-all(bf16[128,2,2048]{0,2,1:T(8,128)(2,1)S(1)} %bitcast.387), channel_id=1, replica_groups=mesh['seq'=16,'ch'=2] {'ch'}, dimensions={1} | all-to-all | bytes 2097152 | tf_op jit(solution)/shard_map/all_to_all | solution.py:164
  36.0 3.8 reduce
  41.0 6.4 %all-to-all-start.1 = ((bf16[16,2,8192]{2,1,0:T(2,128)(2,1)}), bf16[16,2,8192]{2,1,0:T(2,128)(2,1)S(1)}, u32[]{:S(2)}, u32[]{:S(2)}) async-start(bf16[16,2,8192]{2,1,0:T(2,128)(2,1)} %reshape.319), calls=%async_computation.1 | async-start | bytes 1048576 | tf_op jit(solution)/shard_map/all_to_all | solution.py:191
  48.8 3.8 reduce.2
  53.8 13.7 %all-to-all-done.1 = bf16[16,2,8192]{2,1,0:T(2,128)(2,1)S(1)} async-done(((bf16[16,2,8192]{2,1,0:T(2,128)(2,1)}), bf16[16,2,8192]{2,1,0:T(2,128)(2,1)S(1)}, u32[]{:S(2)}, u32[]{:S(2)}) %all-to-all-start.1) | async-done | bytes 524320 | tf_op jit(solution)/shard_map/all_to_all | solution.py:191
  67.6 11.8 %all-to-all-start.3 = ((bf16[16,2,8192]{2,1,0:T(2,128)(2,1)}), bf16[16,2,8192]{2,1,0:T(2,128)(2,1)S(1)}, u32[]{:S(2)}, u32[]{:S(2)}) async-start(bf16[16,2,8192]{2,1,0:T(2,128)(2,1)} %reshape.315), calls=%async_computation.3 | async-start | bytes 1048576 | tf_op jit(solution)/shard_map/all_to_all | solution.py:189
  80.5 21.9 %all-to-all-done.3 = bf16[16,2,8192]{2,1,0:T(2,128)(2,1)S(1)} async-done(((bf16[16,2,8192]{2,1,0:T(2,128)(2,1)}), bf16[16,2,8192]{2,1,0:T(2,128)(2,1)S(1)}, u32[]{:S(2)}, u32[]{:S(2)}) %all-to-all-start.3) | async-done | bytes 524320 | tf_op jit(solution)/shard_map/all_to_all | solution.py:189
  105.5 4.1 fusion.71
  109.6 5.1 fusion.56
  114.8 5.2 fusion.65
  119.9 5.5 fusion.58
  125.4 5.1 convolution_add_fusion.4
  130.5 56.4 %all-gather.5.cloned.1.call-done = bf16[4096,2048]{1,0:T(8,128)(2,1)} async-done(((bf16[256,2048]{1,0:T(8,128)(2,1)}), bf16[4096,2048]{1,0:T(8,128)(2,1)}) %all-gather.5.cloned.1.call-update) | async-done | bytes 16777232 | tf_op jit(solution)/shard_map/all_gather | solution.py:167
  186.9 9.4 %fusion.88 = (bf16[16,16,8,128]{3,2,1,0:T(8,128)(2,1)S(1)}, bf16[128,2048]{1,0:T(8,128)(2,1)}) fusion(bf16[128,2048]{1,0:T(8,128)(2,1)S(1)} %copy-done.50, bf16[128,2048]{1,0:T(8,128)(2,1)} %param.14, bf16[128,4096]{1,0:T(8,128)(2,1)} %all-gather.3.cloned.1.call-done, bf16[4096,2048]{1,0:T(8,128)(2,1)} %all-gather.5.cloned.1.call-done), kind=kOutput, calls=%fused_computation.181 | convolution fusion | flops 2149056512 | bytes 19922944 | tf_op jit(solution)/shard_map/dot_general | solution.py:165
  198.1 4.9 reduce.1
  204.2 4.2 all-to-all-start.2
  210.0 6.6 %convolution_subtract_fusion.5 = f32[16,16384]{1,0:T(8,128)} fusion(f32[16,16384]{1,0:T(8,128)} %fusion.56, bf16[16,1,16384]{2,0,1:T(8,128)(2,1)S(1)} %copy.177, s32[16]{0:T(128)S(1)} %iota_multiply_fusion, s32[16384]{0:T(1024)S(1)} %add_select_fusion.2), kind=kOutput, calls=%fused_computation.20 | convolution fusion | flops 27004672 | bytes 2687040 | tf_op jit(solution)/shard_map/ca,am->cm/dot_general | solution.py:32
  216.6 5.1 convolution_add_fusion.1
  221.7 5.2 convolution_subtract_fusion.1
  226.9 2.4 reshape.318
  230.8 4.1 fusion.68
  234.9 4.0 fusion.57
  239.0 4.3 convolution_add_fusion.3
  243.3 4.1 convolution_subtract_fusion.4
  247.5 8.8 %subtract_bitcast_fusion.6 = (f32[2,8,128,128]{3,1,2,0:T(8,128)}, f32[2,8,128,128]{3,1,2,0:T(8,128)}, f32[2,8,128,128]{3,1,2,0:T(8,128)}, f32[2,8,128,128]{3,1,2...) fusion(f32[16,16384]{1,0:T(8,128)S(1)} %copy-done.16, ...), kind=kOutput, calls=%fused_computation.139 | convolution fusion | flops 38538752 | bytes 24707072 | tf_op jit(solution)/shard_map/ca,am->cm/dot_general | solution.py:32
  291.7 2.8 multiply_add_fusion.2
  307.4 1.9 fusion.202
  322.0 2.1 convolution_subtract_fusion.15
  347.9 5.7 add_bitcast_fusion.4
  357.5 4.4 fusion.4
  365.7 4.8 fusion.9
  372.6 4.5 fusion.3
  377.1 4.7 fusion.8
  381.9 3.0 copy.165
  384.9 6.0 %all-to-all-start.4 = ((f32[2,16,16384]{2,0,1:T(2,128)}), f32[2,16,16384]{2,0,1:T(2,128)S(1)}, u32[]{:S(2)}, u32[]{:S(2)}) async-start(f32[2,16,16384]{2,0,1:T(2,128)} %copy.165), calls=%async_computation.4 | async-start | bytes 4194304 | tf_op jit(solution)/shard_map/all_to_all | solution.py:202
  391.1 2.3 collective-permute-start.3
  394.3 3.5 collective-permute-start.2
  398.6 2.0 maximum_bitcast_fusion.3
  401.7 30.2 %all-to-all-done.4 = f32[2,16,16384]{2,0,1:T(2,128)S(1)} async-done(((f32[2,16,16384]{2,0,1:T(2,128)}), f32[2,16,16384]{2,0,1:T(2,128)S(1)}, u32[]{:S(2)}, u32[]{:S(2)}) %all-to-all-start.4) | async-done | bytes 2097184 | tf_op jit(solution)/shard_map/all_to_all | solution.py:202
  431.9 2.8 reshape.304
  434.7 2.8 copy.296
  441.3 14.9 %fusion.11 = f32[1,128,2048]{2,0,1:T(1,128)S(1)} fusion(bf16[1,255,2048]{2,1,0:T(8,128)(2,1)S(1)} %copy-done.48, bf16[128,1,2048]{2,0,1:T(8,128)(2,1)S(1)} %bitcast.394), kind=kOutput, calls=%fused_computation.47 | convolution fusion | flops 67108864 | bytes 2617344 | tf_op jit(solution)/shard_map/conv_general_dilated | solution.py:123
  457.9 5.2 rev.7
  463.2 14.8 %convolution_convert_fusion = bf16[1,128,2048]{2,0,1:T(2,128)(2,1)S(1)} fusion(bf16[1,255,2048]{2,1,0:T(8,128)(2,1)S(1)} %maximum_bitcast_fusion, bf16[128,1,2048]{2,0,1:T(8,128)(2,1)S(1)} %bitcast.335), kind=kOutput, calls=%fused_computation.43 | convolution fusion | flops 67371008 | bytes 2093056 | tf_op jit(solution)/shard_map/conv_general_dilated | solution.py:123
  479.7 2.5 fusion.15
  482.6 68.9 %psum.14 = f32[7,2048]{1,0:T(8,128)S(1)} all-reduce(f32[7,2048]{1,0:T(8,128)S(1)} %rev.6), channel_id=1, replica_groups=mesh['seq'=16,'ch'=2] {'seq'}, use_global_device_ids=true, to_apply=%region_0.1 | all-reduce | flops 14336 | bytes 114688 | tf_op jit(solution)/shard_map/psum | solution.py:223
  552.2 21.0 %all-reduce.2.cloned.1.call-done = f32[128,2048]{1,0:T(8,128)} async-done(((f32[128,2048]{1,0:T(8,128)}), f32[128,2048]{1,0:T(8,128)}) %all-reduce.2.cloned.1.call-update) | async-done | bytes 1048592 | tf_op jit(solution)/shard_map/psum | solution.py:223
  573.2 2.3 broadcast_multiply_fusion
  (243 shorter events, 126.9 us)
Async XLA Ops:
  7.2 456.0 %copy-start = (bf16[128,2048]{1,0:T(8,128)(2,1)S(1)}, bf16[128,2048]{1,0:T(8,128)(2,1)}, u32[]{:S(2)}) copy-start(bf16[128,2048]{1,0:T(8,128)(2,1)} %param.21) | copy-start | bytes 1572868
  7.2 123.3 %all-gather.3.cloned.1.call-start = ((), (), s32[]{:S(2)}) async-start(), calls=%async_computation.5 | async-start | bytes 1572864 | tf_op jit(solution)/shard_map/all_gather | solution.py:163
  7.9 179.0 %all-gather.5.cloned.1.call-start = ((), (), s32[]{:S(2)}) async-start(), calls=%async_computation.6 | async-start | bytes 17825792 | tf_op jit(solution)/shard_map/all_gather | solution.py:167
  35.5 11.9 %copy-start.44 = (bf16[128,2048]{1,0:T(8,128)(2,1)S(1)}, bf16[128,2048]{1,0:T(8,128)(2,1)}, u32[]{:S(2)}) copy-start(bf16[128,2048]{1,0:T(8,128)(2,1)} %param.15) | copy-start | bytes 1572868
  41.0 26.6 %all-to-all-start.1 = ((bf16[16,2,8192]{2,1,0:T(2,128)(2,1)}), bf16[16,2,8192]{2,1,0:T(2,128)(2,1)S(1)}, u32[]{:S(2)}, u32[]{:S(2)}) async-start(bf16[16,2,8192]{2,1,0:T(2,128)(2,1)} %reshape.319), calls=%async_computation.1 | async-start | bytes 1048576 | tf_op jit(solution)/shard_map/all_to_all | solution.py:191
  67.6 34.9 %all-to-all-start.3 = ((bf16[16,2,8192]{2,1,0:T(2,128)(2,1)}), bf16[16,2,8192]{2,1,0:T(2,128)(2,1)S(1)}, u32[]{:S(2)}, u32[]{:S(2)}) async-start(bf16[16,2,8192]{2,1,0:T(2,128)(2,1)} %reshape.315), calls=%async_computation.3 | async-start | bytes 1048576 | tf_op jit(solution)/shard_map/all_to_all | solution.py:189
  119.9 67.0 %copy-start.50 = (bf16[128,2048]{1,0:T(8,128)(2,1)S(1)}, bf16[128,2048]{1,0:T(8,128)(2,1)}, u32[]{:S(2)}) copy-start(bf16[128,2048]{1,0:T(8,128)(2,1)} %param.13) | copy-start | bytes 1572868
  204.2 22.7 %all-to-all-start.2 = ((bf16[16,2,8192]{2,1,0:T(2,128)(2,1)}), bf16[16,2,8192]{2,1,0:T(2,128)(2,1)}, u32[]{:S(2)}, u32[]{:S(2)}) async-start(bf16[16,2,8192]{2,1,0:T(2,128)(2,1)} %reshape.317), calls=%async_computation.2 | async-start | bytes 1048576 | tf_op jit(solution)/shard_map/all_to_all | solution.py:190
  208.4 8.2 %copy-start.35 = (f32[16,16384]{1,0:T(8,128)S(1)}, f32[16,16384]{1,0:T(8,128)}, u32[]{:S(2)}) copy-start(f32[16,16384]{1,0:T(8,128)} %fusion.65) | copy-start | bytes 3145732
  210.0 11.7 %copy-start.34 = (f32[16,16384]{1,0:T(8,128)S(1)}, f32[16,16384]{1,0:T(8,128)}, u32[]{:S(2)}) copy-start(f32[16,16384]{1,0:T(8,128)} %fusion.58) | copy-start | bytes 3145732
  234.9 12.5 %copy-start.22 = (f32[16,16384]{1,0:T(8,128)S(1)}, f32[16,16384]{1,0:T(8,128)}, u32[]{:S(2)}) copy-start(f32[16,16384]{1,0:T(8,128)} %convolution_subtract_fusion.1) | copy-start | bytes 3145732
  239.0 8.4 %copy-start.15 = (f32[16,16384]{1,0:T(8,128)S(1)}, f32[16,16384]{1,0:T(8,128)}, u32[]{:S(2)}) copy-start(f32[16,16384]{1,0:T(8,128)} %fusion.96) | copy-start | bytes 3145732
  239.0 8.4 %copy-start.16 = (f32[16,16384]{1,0:T(8,128)S(1)}, f32[16,16384]{1,0:T(8,128)}, u32[]{:S(2)}) copy-start(f32[16,16384]{1,0:T(8,128)} %convolution_add_fusion.4) | copy-start | bytes 3145732
  239.0 8.4 %copy-start.19 = (f32[16,16384]{1,0:T(8,128)S(1)}, f32[16,16384]{1,0:T(8,128)}, u32[]{:S(2)}) copy-start(f32[16,16384]{1,0:T(8,128)} %fusion.110) | copy-start | bytes 3145732
  239.0 8.4 %copy-start.20 = (f32[16,16384]{1,0:T(8,128)S(1)}, f32[16,16384]{1,0:T(8,128)}, u32[]{:S(2)}) copy-start(f32[16,16384]{1,0:T(8,128)} %convolution_subtract_fusion.5) | copy-start | bytes 3145732
  239.0 8.4 %copy-start.21 = (f32[16,16384]{1,0:T(8,128)S(1)}, f32[16,16384]{1,0:T(8,128)}, u32[]{:S(2)}) copy-start(f32[16,16384]{1,0:T(8,128)} %convolution_add_fusion.1) | copy-start | bytes 3145732
  257.5 3.5 copy-start.25
  263.7 1.9 copy-start.29
  265.6 1.8 copy-start.24
  270.1 3.0 copy-start.5
  270.1 1.8 copy-start.23
  274.7 1.8 copy-start.30
  276.5 1.8 copy-start.26
  278.3 1.8 copy-start.18
  281.3 3.5 copy-start.17
  288.8 1.8 copy-start.43
  289.7 2.0 copy-start.39
  298.0 1.9 copy-start.14
  301.1 3.4 copy-start.13
  307.4 1.9 copy-start.32
  309.2 1.8 copy-start.12
  313.8 3.0 copy-start.3
  313.8 1.8 copy-start.11
  318.4 1.8 copy-start.33
  320.2 1.8 copy-start.27
  322.0 2.1 copy-start.10
  325.3 3.5 copy-start.9
  333.7 2.0 copy-start.38
  339.6 2.0 copy-start.2
  384.9 6.1 %copy-start.47 = (bf16[128,2048]{1,0:T(8,128)(2,1)S(1)}, bf16[128,2048]{1,0:T(8,128)(2,1)}, u32[]{:S(2)}) copy-start(bf16[128,2048]{1,0:T(8,128)(2,1)} %param.17) | copy-start | bytes 1572868
  384.9 47.0 %all-to-all-start.4 = ((f32[2,16,16384]{2,0,1:T(2,128)}), f32[2,16,16384]{2,0,1:T(2,128)S(1)}, u32[]{:S(2)}, u32[]{:S(2)}) async-start(f32[2,16,16384]{2,0,1:T(2,128)} %copy.165), calls=%async_computation.4 | async-start | bytes 4194304 | tf_op jit(solution)/shard_map/all_to_all | solution.py:202
  390.9 182.2 %all-reduce.2.cloned.1.call-start = ((), (), s32[]{:S(2)}) async-start(), calls=%async_computation.7 | async-start | bytes 2097152 | tf_op jit(solution)/shard_map/psum | solution.py:223
  391.1 9.5 %collective-permute-start.3 = (bf16[127,2048]{1,0:T(8,128)(2,1)S(1)}, bf16[127,2048]{1,0:T(8,128)(2,1)S(1)}, u32[]{:S(2)}, u32[]{:S(2)}) collective-permute-start(bf16[127,2048]{1,0:T(8,128)(2,1)S(1)} %slice.29), channel_id=1, source_target_pairs={{0,2},{2,4},{4,6},{6,8},{8,10},{10,12},{12,14},{14,16},{16,18},{18... | collective-permute-start | bytes 1560584 | tf_op jit(solution)/shard_map/ppermute | solution.py:15
  394.3 4.4 collective-permute-start.2
  437.7 3.6 copy-start.48
  440.0 23.0 %collective-permute-start = (bf16[127,2048]{1,0:T(8,128)(2,1)S(1)}, bf16[127,2048]{1,0:T(8,128)(2,1)S(1)}, u32[]{:S(2)}, u32[]{:S(2)}) collective-permute-start(bf16[127,2048]{1,0:T(8,128)(2,1)S(1)} %bitcast.393), channel_id=1, source_target_pairs={{2,0},{4,2},{6,4},{8,6},{10,8},{12,10},{14,12},{16,14},{18,16},{20... | collective-permute-start | bytes 1560584 | tf_op jit(solution)/shard_map/ppermute | solution.py:15
  463.2 16.6 %copy-start.49 = (bf16[1,134,2048]{2,1,0:T(8,128)(2,1)S(1)}, bf16[1,134,2048]{2,1,0:T(8,128)(2,1)}, u32[]{:S(2)}) copy-start(bf16[1,134,2048]{2,1,0:T(8,128)(2,1)} %maximum_bitcast_fusion.3) | copy-start | bytes 1646596
  478.4 97.0 %collective-permute-start.1 = (bf16[6,2048]{1,0:T(8,128)(2,1)S(1)}, bf16[6,2048]{1,0:T(8,128)(2,1)S(1)}, u32[]{:S(2)}, u32[]{:S(2)}) collective-permute-start(bf16[6,2048]{1,0:T(8,128)(2,1)S(1)} %bitcast.397), channel_id=1, source_target_pairs={{2,0},{4,2},{6,4},{8,6},{10,8},{12,10},{14,12},{16,14},{18,16},{20... | collective-permute-start | bytes 73736 | tf_op jit(solution)/shard_map/ppermute | solution.py:15
  (17 other events, 22.9 us)
Sparse Core Ops, SparseCore 0:
  9.5 29.1 all-gather.2
  41.5 145.4 all-gather.4
  463.2 109.9 all-reduce.1
where the time goes:
time: 593 us; the launch traced here: 585 us
  matrix products  200 us (34%)
  waiting for transfers between devices  145 us (24%)
  blocking collectives  93 us (16%)
  local copies, waits for them, and re-layouts  73.2 us (12%)
  starting transfers between devices  37 us (6%)
  other arithmetic  21.5 us (4%)
  between operations  15.2 us (3%)
    dot_general x66, matrix products, multiply(): return jnp.einsum(pattern, left, right, precision=ACCURATE)  154 us
    psum x1, blocking collectives, per_device(): sum_medium, sum_short = lax.psum((partial_medium, partial_short), 'seq')  68.9 us
    all_gather x1, waiting for transfers between devices, per_device(): lax.all_gather(aligned, 'seq', axis=0, tiled=True)  56.4 us
    conv_general_dilated x4, matrix products, depthwise(): lax.conv_general_dilated(signal.astype(jnp.float32)[None], kernel.astype(...  32.9 us
    unnamed x135, local copies, waits for them, and re-layouts  31.9 us
    all_to_all x1, waiting for transfers between devices, per_device(): lax.all_to_all(jnp.stack(results), 'seq', split_axis=1, concat_axis=1, ti...  30.2 us
    all_to_all x1, blocking collectives, per_device(): lax.all_to_all(out_weight, 'ch', split_axis=1, concat_axis=0, tiled=True)  24.2 us
    all_to_all x1, waiting for transfers between devices, per_device(): lax.all_to_all(to_blocks(product), 'seq', split_axis=0, concat_axis=0, ti...  21.9 us
  transfers between devices with their start and end apart: 11, of which 6 were waited for; matrix products, arithmetic and copies ran while one was open for 19% of the time, Pallas kernels for 0%

commit v1 on v0

--- a/solution.py
+++ b/solution.py
@@ -7,6 +7,24 @@
 SHORT = 7
 MEDIUM = 128
 ACCURATE = lax.Precision.HIGH
+
+
+def collect(shard, axis, dim):
+    ways, here, step = (lax.axis_size(axis), lax.axis_index(axis), shard.shape[dim])
+    lengths = [n * ways if d == dim else n for d, n in enumerate(shard.shape)]
+    full = lax.dynamic_update_slice_in_dim(
+        jnp.zeros(lengths, shard.dtype), shard, here * step, axis=dim
+    )
+    going_up = going_down = shard
+    for far in range(1, ways // 2 + 1):
+        going_up = lax.ppermute(going_up, axis, [(d, (d + 1) % ways) for d in range(ways)])
+        full = lax.dynamic_update_slice_in_dim(full, going_up, (here - far) % ways * step, axis=dim)
+        if 2 * far < ways:
+            going_down = lax.ppermute(going_down, axis, [(d, (d - 1) % ways) for d in range(ways)])
+            full = lax.dynamic_update_slice_in_dim(
+                full, going_down, (here + far) % ways * step, axis=dim
+            )
+    return full
 
 
 def from_behind(value, axis, steps):
@@ -162,11 +180,7 @@
     )
     features = lax.all_gather(out_grad, "ch", axis=1, tiled=True)
     aligned = lax.all_to_all(out_weight, "ch", split_axis=1, concat_axis=0, tiled=True)
-    hidden = jnp.dot(
-        features,
-        lax.all_gather(aligned, "seq", axis=0, tiled=True),
-        preferred_element_type=jnp.float32,
-    )
+    hidden = jnp.dot(features, collect(aligned, "seq", 0), preferred_element_type=jnp.float32)
     grad_outer = (hidden * long_out.astype(jnp.float32)).astype(jnp.bfloat16)
     long_grad = (hidden * outer_gate.astype(jnp.float32)).astype(jnp.bfloat16)
     product = (inner_gate.astype(jnp.float32) * medium_out.astype(jnp.float32)).astype(jnp.bfloat16)

time: 593 us -> 665 us (1.12)
  starting transfers between devices: 37 us -> 128 us
  waiting for transfers between devices: 145 us -> 58.3 us
  local copies, waits for them, and re-layouts: 73.2 us -> 118 us
  matrix products: 200 us -> 221 us
    ppermute x0 -> x15, starting transfers between devices: none -> 77 us  [the longest x8 48.4 us: collect(): lax.ppermute(going_up, axis, [(d, (d + 1) % ways) for d in range(ways)])]
    all_gather x1 -> x0, waiting for transfers between devices: 56.4 us -> none  [per_device(): lax.all_gather(aligned, 'seq', axis=0, tiled=True)]
    dynamic_update_slice x0 -> x16, local copies, waits for them, and re-layouts: none -> 25.8 us  [the longest x8 13.5 us: collect(): lax.dynamic_update_slice_in_dim(full, going_up, (here - far) % ways * ste...]
    all_to_all x1, waiting for transfers between devices: 21.9 us -> 0.01 us  [per_device(): lax.all_to_all(to_blocks(product), 'seq', split_axis=0, concat_axis=0, ti...]
    dot_general x66, matrix products: 154 us -> 170 us  [multiply(): return jnp.einsum(pattern, left, right, precision=ACCURATE)]
    all_to_all x1, waiting for transfers between devices: 13.7 us -> 0.01 us  [per_device(): lax.all_to_all(to_blocks(long_filter), 'seq', split_axis=0, concat_axis=0...]
    ppermute x0 -> x15, waiting for transfers between devices: none -> 12.7 us  [the longest x8 12.7 us: collect(): lax.ppermute(going_up, axis, [(d, (d + 1) % ways) for d in range(ways)])]
    unnamed x135 -> x60, local copies, waits for them, and re-layouts: 31.9 us -> 44.6 us
  transfers between devices with their start and end apart: 11 -> 25, of which waited for: 6 -> 4; matrix products, arithmetic and copies ran while one was open for 19% -> 24% of each run, Pallas kernels for 0% -> 0%
where the time goes in v1:
time: 665 us; the launch traced here: 655 us
  matrix products  221 us (33%)
  starting transfers between devices  128 us (19%)
  local copies, waits for them, and re-layouts  118 us (18%)
  blocking collectives  88.6 us (13%)
  waiting for transfers between devices  58.3 us (9%)
  other arithmetic  25.8 us (4%)
  between operations  15.6 us (2%)
    dot_general x66, matrix products, multiply(): return jnp.einsum(pattern, left, right, precision=ACCURATE)  170 us
    psum x1, blocking collectives, per_device(): sum_medium, sum_short = lax.psum((partial_medium, partial_short), 'seq')  70.9 us
    ppermute x8, starting transfers between devices, collect(): lax.ppermute(going_up, axis, [(d, (d + 1) % ways) for d in range(ways)])  48.4 us
    unnamed x60, local copies, waits for them, and re-layouts  44.6 us
    conv_general_dilated x4, matrix products, depthwise(): lax.conv_general_dilated(signal.astype(jnp.float32)[None], kernel.astype(...  34.5 us
    ppermute x7, starting transfers between devices, collect(): lax.ppermute(going_down, axis, [(d, (d - 1) % ways) for d in range(ways)])  28.6 us
    all_to_all x1, waiting for transfers between devices, per_device(): lax.all_to_all(jnp.stack(results), 'seq', split_axis=1, concat_axis=1, ti...  26 us
    psum x1, waiting for transfers between devices, per_device(): sum_medium, sum_short = lax.psum((partial_medium, partial_short), 'seq')  18.7 us
  transfers between devices with their start and end apart: 25, of which 4 were waited for; matrix products, arithmetic and copies ran while one was open for 24% of the time, Pallas kernels for 0%

profile of v1, /device:TPU:0, one launch (start us, length us, event | category | flops | bytes accessed | tf_op | source)
XLA Modules:
  0.0 654.8 jit_solution(12147143209121941803)
XLA Ops:
  8.9 17.7 %all_to_all.63 = bf16[128,2,2048]{0,2,1:T(8,128)(2,1)S(1)} all-to-all(bf16[128,2,2048]{0,2,1:T(8,128)(2,1)S(1)} %bitcast.385), channel_id=1, replica_groups=mesh['seq'=16,'ch'=2] {'ch'}, dimensions={1} | all-to-all | bytes 2097152 | tf_op jit(solution)/shard_map/all_to_all | solution.py:182
  27.1 4.4 collective-permute-start.1
  31.5 12.7 %collective-permute-done = bf16[256,2048]{1,0:T(8,128)(2,1)} collective-permute-done((bf16[256,2048]{1,0:T(8,128)(2,1)S(1)}, bf16[256,2048]{1,0:T(8,128)(2,1)}, u32[]{:S(2)}, u32[]{:S(2)}) %collective-permute-start) | collective-permute-done | bytes 1048608 | tf_op jit(solution)/shard_map/ppermute | solution.py:20
  44.2 7.6 %collective-permute-start.2 = (bf16[256,2048]{1,0:T(8,128)(2,1)}, bf16[256,2048]{1,0:T(8,128)(2,1)}, u32[]{:S(2)}, u32[]{:S(2)}) collective-permute-start(bf16[256,2048]{1,0:T(8,128)(2,1)} %collective-permute-done), channel_id=1, source_target_pairs={{0,2},{2,4},{4,6},{6,8},{8,10},{10,12},{12,14},{14,16},{16,18},{18... | collective-permute-start | bytes 3145736 | tf_op jit(solution)/shard_map/ppermute | solution.py:20
  54.0 3.8 reduce.2
  59.0 7.2 %all-to-all-start.3 = ((bf16[16,2,8192]{2,1,0:T(2,128)(2,1)}), bf16[16,2,8192]{2,1,0:T(2,128)(2,1)S(1)}, u32[]{:S(2)}, u32[]{:S(2)}) async-start(bf16[16,2,8192]{2,1,0:T(2,128)(2,1)} %reshape.315), calls=%async_computation.3 | async-start | bytes 1048576 | tf_op jit(solution)/shard_map/all_to_all | solution.py:203
  66.1 4.4 collective-permute-start.3
  74.5 4.6 reduce
  81.3 14.6 %all-to-all-start.1 = ((bf16[16,2,8192]{2,1,0:T(2,128)(2,1)}), bf16[16,2,8192]{2,1,0:T(2,128)(2,1)}, u32[]{:S(2)}, u32[]{:S(2)}) async-start(bf16[16,2,8192]{2,1,0:T(2,128)(2,1)} %reshape.319), calls=%async_computation.1 | async-start | bytes 1048576 | tf_op jit(solution)/shard_map/all_to_all | solution.py:205
  96.0 4.3 collective-permute-start.5
  105.3 6.0 broadcast_in_dim.16
  116.3 4.1 fusion.65
  120.4 10.9 %collective-permute-start.7 = (bf16[256,2048]{1,0:T(8,128)(2,1)}, bf16[256,2048]{1,0:T(8,128)(2,1)S(1)}, u32[]{:S(2)}, u32[]{:S(2)}) collective-permute-start(bf16[256,2048]{1,0:T(8,128)(2,1)} %collective-permute-done.5), channel_id=1, source_target_pairs={{0,30},{2,0},{4,2},{6,4},{8,6},{10,8},{12,10},{14,12},{16,14},{18,... | collective-permute-start | bytes 3145736 | tf_op jit(solution)/shard_map/ppermute | solution.py:23
  131.4 5.1 fusion.58
  136.6 5.2 fusion.71
  141.8 5.1 fusion.56
  146.9 4.0 convolution_add_fusion.1
  151.0 4.5 collective-permute-start.9
  156.9 8.8 %collective-permute-start.10 = (bf16[256,2048]{1,0:T(8,128)(2,1)S(1)}, bf16[256,2048]{1,0:T(8,128)(2,1)S(1)}, u32[]{:S(2)}, u32[]{:S(2)}) collective-permute-start(bf16[256,2048]{1,0:T(8,128)(2,1)S(1)} %collective-permute-done.8), channel_id=1, source_target_pairs={{0,2},{2,4},{4,6},{6,8},{8,10},{10,12},{12,14},{14,16},{16,18},{18... | collective-permute-start | bytes 3145736 | tf_op jit(solution)/shard_map/ppermute | solution.py:20
  176.4 14.5 %collective-permute-start.12 = (bf16[256,2048]{1,0:T(8,128)(2,1)S(1)}, bf16[256,2048]{1,0:T(8,128)(2,1)S(1)}, u32[]{:S(2)}, u32[]{:S(2)}) collective-permute-start(bf16[256,2048]{1,0:T(8,128)(2,1)S(1)} %collective-permute-done.10), channel_id=1, source_target_pairs={{0,2},{2,4},{4,6},{6,8},{8,10},{10,12},{12,14},{14,16},{16,18},{18... | collective-permute-start | bytes 3145736 | tf_op jit(solution)/shard_map/ppermute | solution.py:20
  200.1 16.8 %collective-permute-start.14 = (bf16[256,2048]{1,0:T(8,128)(2,1)S(1)}, bf16[256,2048]{1,0:T(8,128)(2,1)S(1)}, u32[]{:S(2)}, u32[]{:S(2)}) collective-permute-start(bf16[256,2048]{1,0:T(8,128)(2,1)S(1)} %collective-permute-done.12), channel_id=1, source_target_pairs={{0,2},{2,4},{4,6},{6,8},{8,10},{10,12},{12,14},{14,16},{16,18},{18... | collective-permute-start | bytes 3145736 | tf_op jit(solution)/shard_map/ppermute | solution.py:20
  223.2 11.8 %multiply_convert_fusion = (bf16[128,2048]{0,1:T(8,128)(2,1)}, bf16[128,2048]{0,1:T(8,128)(2,1)}) fusion(bf16[128,2048]{0,1:T(8,128)(2,1)} %copy.156, bf16[128,2048]{0,1:T(8,128)(2,1)S(1)} %copy-done.12, bf16[4096,2048]{1,0:T(8,128)(2,1)} %constant_dynamic-update-slice_fusion, bf16[128,4096]{1,0:T(8,128)(2,1)} %all-gather.2.cloned.1.call-done), kind=kOutput, calls=%fused_computation.155 | convolution fusion | flops 2149056512 | bytes 19922944 | tf_op jit(solution)/shard_map/dot_general | solution.py:183
  238.0 4.9 reduce.1
  244.1 14.7 %all-to-all-start.2 = ((bf16[16,2,8192]{2,1,0:T(2,128)(2,1)}), bf16[16,2,8192]{2,1,0:T(2,128)(2,1)S(1)}, u32[]{:S(2)}, u32[]{:S(2)}) async-start(bf16[16,2,8192]{2,1,0:T(2,128)(2,1)} %reshape.317), calls=%async_computation.2 | async-start | bytes 1048576 | tf_op jit(solution)/shard_map/all_to_all | solution.py:204
  260.2 6.5 convolution_add_fusion.4
  266.7 6.5 convolution_subtract_fusion.1
  273.2 6.5 convolution_subtract_fusion.5
  283.6 4.0 fusion.57
  287.6 4.1 fusion.68
  292.7 4.3 convolution_subtract_fusion.4
  297.0 4.1 convolution_add_fusion.3
  301.1 11.2 %subtract_bitcast_fusion.6 = (f32[2,8,128,128]{3,1,2,0:T(8,128)}, f32[2,8,128,128]{3,1,2,0:T(8,128)}, f32[2,8,128,128]{3,1,2,0:T(8,128)}, f32[2,8,128,128]{3,1,2...) fusion(f32[16,16384]{1,0:T(8,128)} %convolution_add_fusion.4, ...), kind=kOutput, calls=%fused_computation.140 | convolution fusion | flops 38538752 | bytes 24707072 | tf_op jit(solution)/shard_map/ca,am->cm/dot_general | solution.py:50
  351.3 5.0 multiply_add_fusion.3
  368.1 3.1 convolution_subtract_fusion.8
  400.3 3.5 multiply_add_fusion.2
  414.8 5.7 add_bitcast_fusion.4
  422.9 4.6 fusion.9
  431.3 4.4 fusion.4
  439.6 4.5 fusion.8
  444.1 4.7 fusion.3
  451.9 6.0 all-to-all-start.4
  462.2 3.5 collective-permute-start.17
  472.8 26.0 %all-to-all-done.4 = f32[2,16,16384]{2,0,1:T(2,128)S(1)} async-done(((f32[2,16,16384]{2,0,1:T(2,128)}), f32[2,16,16384]{2,0,1:T(2,128)S(1)}, u32[]{:S(2)}, u32[]{:S(2)}) %all-to-all-start.4) | async-done | bytes 2097184 | tf_op jit(solution)/shard_map/all_to_all | solution.py:216
  508.5 16.4 %fusion.11 = f32[1,128,2048]{2,0,1:T(1,128)S(1)} fusion(bf16[1,255,2048]{2,1,0:T(8,128)(2,1)} %maximum_bitcast_fusion.1, bf16[128,1,2048]{2,0,1:T(8,128)(2,1)} %bitcast.64), kind=kOutput, calls=%fused_computation.48 | convolution fusion | flops 67108864 | bytes 2617344 | tf_op jit(solution)/shard_map/conv_general_dilated | solution.py:141
  525.2 5.2 rev.7
  532.9 14.8 %convolution_convert_fusion = bf16[1,128,2048]{2,0,1:T(2,128)(2,1)S(1)} fusion(bf16[1,255,2048]{2,1,0:T(8,128)(2,1)S(1)} %maximum_bitcast_fusion, bf16[128,1,2048]{2,0,1:T(8,128)(2,1)S(1)} %bitcast.331), kind=kOutput, calls=%fused_computation.44 | convolution fusion | flops 67371008 | bytes 2093056 | tf_op jit(solution)/shard_map/conv_general_dilated | solution.py:141
  552.4 70.9 %psum.14 = f32[7,2048]{1,0:T(8,128)S(1)} all-reduce(f32[7,2048]{1,0:T(8,128)S(1)} %rev.6), channel_id=1, replica_groups=mesh['seq'=16,'ch'=2] {'seq'}, use_global_device_ids=true, to_apply=%region_0.1 | all-reduce | flops 14336 | bytes 114688 | tf_op jit(solution)/shard_map/psum | solution.py:237
  623.9 18.7 %all-reduce.2.cloned.1.call-done = f32[128,2048]{1,0:T(8,128)} async-done(((f32[128,2048]{1,0:T(8,128)}), f32[128,2048]{1,0:T(8,128)}) %all-reduce.2.cloned.1.call-update) | async-done | bytes 1048592 | tf_op jit(solution)/shard_map/psum | solution.py:237
  (212 shorter events, 197.4 us)
Async XLA Ops:
  7.2 525.7 %copy-start = (bf16[128,2048]{1,0:T(8,128)(2,1)S(1)}, bf16[128,2048]{1,0:T(8,128)(2,1)}, u32[]{:S(2)}) copy-start(bf16[128,2048]{1,0:T(8,128)(2,1)} %param.21) | copy-start | bytes 1572868
  27.0 17.2 %collective-permute-start = (bf16[256,2048]{1,0:T(8,128)(2,1)S(1)}, bf16[256,2048]{1,0:T(8,128)(2,1)}, u32[]{:S(2)}, u32[]{:S(2)}) collective-permute-start(bf16[256,2048]{1,0:T(8,128)(2,1)S(1)} %bitcast.365), channel_id=1, source_target_pairs={{0,2},{2,4},{4,6},{6,8},{8,10},{10,12},{12,14},{14,16},{16,18},{18... | collective-permute-start | bytes 3145736 | tf_op jit(solution)/shard_map/ppermute | solution.py:20
  27.1 39.0 %collective-permute-start.1 = (bf16[256,2048]{1,0:T(8,128)(2,1)S(1)}, bf16[256,2048]{1,0:T(8,128)(2,1)}, u32[]{:S(2)}, u32[]{:S(2)}) collective-permute-start(bf16[256,2048]{1,0:T(8,128)(2,1)S(1)} %bitcast.366), channel_id=1, source_target_pairs={{0,30},{2,0},{4,2},{6,4},{8,6},{10,8},{12,10},{14,12},{16,14},{18,... | collective-permute-start | bytes 3145736 | tf_op jit(solution)/shard_map/ppermute | solution.py:23
  44.2 26.3 %collective-permute-start.2 = (bf16[256,2048]{1,0:T(8,128)(2,1)}, bf16[256,2048]{1,0:T(8,128)(2,1)}, u32[]{:S(2)}, u32[]{:S(2)}) collective-permute-start(bf16[256,2048]{1,0:T(8,128)(2,1)} %collective-permute-done), channel_id=1, source_target_pairs={{0,2},{2,4},{4,6},{6,8},{8,10},{10,12},{12,14},{14,16},{16,18},{18... | collective-permute-start | bytes 3145736 | tf_op jit(solution)/shard_map/ppermute | solution.py:20
  59.0 22.4 %all-to-all-start.3 = ((bf16[16,2,8192]{2,1,0:T(2,128)(2,1)}), bf16[16,2,8192]{2,1,0:T(2,128)(2,1)S(1)}, u32[]{:S(2)}, u32[]{:S(2)}) async-start(bf16[16,2,8192]{2,1,0:T(2,128)(2,1)} %reshape.315), calls=%async_computation.3 | async-start | bytes 1048576 | tf_op jit(solution)/shard_map/all_to_all | solution.py:203
  66.1 29.9 %collective-permute-start.3 = (bf16[256,2048]{1,0:T(8,128)(2,1)}, bf16[256,2048]{1,0:T(8,128)(2,1)}, u32[]{:S(2)}, u32[]{:S(2)}) collective-permute-start(bf16[256,2048]{1,0:T(8,128)(2,1)} %collective-permute-done.1), channel_id=1, source_target_pairs={{0,30},{2,0},{4,2},{6,4},{8,6},{10,8},{12,10},{14,12},{16,14},{18,... | collective-permute-start | bytes 3145736 | tf_op jit(solution)/shard_map/ppermute | solution.py:23
  70.5 29.9 %collective-permute-start.4 = (bf16[256,2048]{1,0:T(8,128)(2,1)}, bf16[256,2048]{1,0:T(8,128)(2,1)}, u32[]{:S(2)}, u32[]{:S(2)}) collective-permute-start(bf16[256,2048]{1,0:T(8,128)(2,1)} %collective-permute-done.2), channel_id=1, source_target_pairs={{0,2},{2,4},{4,6},{6,8},{8,10},{10,12},{12,14},{14,16},{16,18},{18... | collective-permute-start | bytes 3145736 | tf_op jit(solution)/shard_map/ppermute | solution.py:20
  81.3 32.2 %all-to-all-start.1 = ((bf16[16,2,8192]{2,1,0:T(2,128)(2,1)}), bf16[16,2,8192]{2,1,0:T(2,128)(2,1)}, u32[]{:S(2)}, u32[]{:S(2)}) async-start(bf16[16,2,8192]{2,1,0:T(2,128)(2,1)} %reshape.319), calls=%async_computation.1 | async-start | bytes 1048576 | tf_op jit(solution)/shard_map/all_to_all | solution.py:205
  96.0 127.3 %all-gather.2.cloned.1.call-start = ((), (), s32[]{:S(2)}) async-start(), calls=%async_computation.5 | async-start | bytes 1572864 | tf_op jit(solution)/shard_map/all_gather | solution.py:181
  96.0 24.4 %collective-permute-start.5 = (bf16[256,2048]{1,0:T(8,128)(2,1)}, bf16[256,2048]{1,0:T(8,128)(2,1)}, u32[]{:S(2)}, u32[]{:S(2)}) collective-permute-start(bf16[256,2048]{1,0:T(8,128)(2,1)} %collective-permute-done.3), channel_id=1, source_target_pairs={{0,30},{2,0},{4,2},{6,4},{8,6},{10,8},{12,10},{14,12},{16,14},{18,... | collective-permute-start | bytes 3145736 | tf_op jit(solution)/shard_map/ppermute | solution.py:23
  100.4 36.1 %collective-permute-start.6 = (bf16[256,2048]{1,0:T(8,128)(2,1)}, bf16[256,2048]{1,0:T(8,128)(2,1)}, u32[]{:S(2)}, u32[]{:S(2)}) collective-permute-start(bf16[256,2048]{1,0:T(8,128)(2,1)} %collective-permute-done.4), channel_id=1, source_target_pairs={{0,2},{2,4},{4,6},{6,8},{8,10},{10,12},{12,14},{14,16},{16,18},{18... | collective-permute-start | bytes 3145736 | tf_op jit(solution)/shard_map/ppermute | solution.py:20
  120.4 30.5 %collective-permute-start.7 = (bf16[256,2048]{1,0:T(8,128)(2,1)}, bf16[256,2048]{1,0:T(8,128)(2,1)S(1)}, u32[]{:S(2)}, u32[]{:S(2)}) collective-permute-start(bf16[256,2048]{1,0:T(8,128)(2,1)} %collective-permute-done.5), channel_id=1, source_target_pairs={{0,30},{2,0},{4,2},{6,4},{8,6},{10,8},{12,10},{14,12},{16,14},{18,... | collective-permute-start | bytes 3145736 | tf_op jit(solution)/shard_map/ppermute | solution.py:23
  136.5 20.4 %collective-permute-start.8 = (bf16[256,2048]{1,0:T(8,128)(2,1)}, bf16[256,2048]{1,0:T(8,128)(2,1)S(1)}, u32[]{:S(2)}, u32[]{:S(2)}) collective-permute-start(bf16[256,2048]{1,0:T(8,128)(2,1)} %collective-permute-done.6), channel_id=1, source_target_pairs={{0,2},{2,4},{4,6},{6,8},{8,10},{10,12},{12,14},{14,16},{16,18},{18... | collective-permute-start | bytes 3145736 | tf_op jit(solution)/shard_map/ppermute | solution.py:20
  151.0 23.2 %collective-permute-start.9 = (bf16[256,2048]{1,0:T(8,128)(2,1)S(1)}, bf16[256,2048]{1,0:T(8,128)(2,1)S(1)}, u32[]{:S(2)}, u32[]{:S(2)}) collective-permute-start(bf16[256,2048]{1,0:T(8,128)(2,1)S(1)} %collective-permute-done.7), channel_id=1, source_target_pairs={{0,30},{2,0},{4,2},{6,4},{8,6},{10,8},{12,10},{14,12},{16,14},{18,... | collective-permute-start | bytes 3145736 | tf_op jit(solution)/shard_map/ppermute | solution.py:23
  156.9 66.3 %copy-start.12 = (bf16[128,2048]{0,1:T(8,128)(2,1)S(1)}, bf16[128,2048]{0,1:T(8,128)(2,1)}, u32[]{:S(2)}) copy-start(bf16[128,2048]{0,1:T(8,128)(2,1)} %copy.151) | copy-start | bytes 1572868
  156.9 19.5 %collective-permute-start.10 = (bf16[256,2048]{1,0:T(8,128)(2,1)S(1)}, bf16[256,2048]{1,0:T(8,128)(2,1)S(1)}, u32[]{:S(2)}, u32[]{:S(2)}) collective-permute-start(bf16[256,2048]{1,0:T(8,128)(2,1)S(1)} %collective-permute-done.8), channel_id=1, source_target_pairs={{0,2},{2,4},{4,6},{6,8},{8,10},{10,12},{12,14},{14,16},{16,18},{18... | collective-permute-start | bytes 3145736 | tf_op jit(solution)/shard_map/ppermute | solution.py:20
  174.1 24.9 %collective-permute-start.11 = (bf16[256,2048]{1,0:T(8,128)(2,1)S(1)}, bf16[256,2048]{1,0:T(8,128)(2,1)S(1)}, u32[]{:S(2)}, u32[]{:S(2)}) collective-permute-start(bf16[256,2048]{1,0:T(8,128)(2,1)S(1)} %collective-permute-done.9), channel_id=1, source_target_pairs={{0,30},{2,0},{4,2},{6,4},{8,6},{10,8},{12,10},{14,12},{16,14},{18,... | collective-permute-start | bytes 3145736 | tf_op jit(solution)/shard_map/ppermute | solution.py:23
  176.4 23.6 %collective-permute-start.12 = (bf16[256,2048]{1,0:T(8,128)(2,1)S(1)}, bf16[256,2048]{1,0:T(8,128)(2,1)S(1)}, u32[]{:S(2)}, u32[]{:S(2)}) collective-permute-start(bf16[256,2048]{1,0:T(8,128)(2,1)S(1)} %collective-permute-done.10), channel_id=1, source_target_pairs={{0,2},{2,4},{4,6},{6,8},{8,10},{10,12},{12,14},{14,16},{16,18},{18... | collective-permute-start | bytes 3145736 | tf_op jit(solution)/shard_map/ppermute | solution.py:20
  199.0 22.1 %collective-permute-start.13 = (bf16[256,2048]{1,0:T(8,128)(2,1)S(1)}, bf16[256,2048]{1,0:T(8,128)(2,1)S(1)}, u32[]{:S(2)}, u32[]{:S(2)}) collective-permute-start(bf16[256,2048]{1,0:T(8,128)(2,1)S(1)} %collective-permute-done.11), channel_id=1, source_target_pairs={{0,30},{2,0},{4,2},{6,4},{8,6},{10,8},{12,10},{14,12},{16,14},{18,... | collective-permute-start | bytes 3145736 | tf_op jit(solution)/shard_map/ppermute | solution.py:23
  200.1 22.1 %collective-permute-start.14 = (bf16[256,2048]{1,0:T(8,128)(2,1)S(1)}, bf16[256,2048]{1,0:T(8,128)(2,1)S(1)}, u32[]{:S(2)}, u32[]{:S(2)}) collective-permute-start(bf16[256,2048]{1,0:T(8,128)(2,1)S(1)} %collective-permute-done.12), channel_id=1, source_target_pairs={{0,2},{2,4},{4,6},{6,8},{8,10},{10,12},{12,14},{14,16},{16,18},{18... | collective-permute-start | bytes 3145736 | tf_op jit(solution)/shard_map/ppermute | solution.py:20
  244.1 35.7 %all-to-all-start.2 = ((bf16[16,2,8192]{2,1,0:T(2,128)(2,1)}), bf16[16,2,8192]{2,1,0:T(2,128)(2,1)S(1)}, u32[]{:S(2)}, u32[]{:S(2)}) async-start(bf16[16,2,8192]{2,1,0:T(2,128)(2,1)} %reshape.317), calls=%async_computation.2 | async-start | bytes 1048576 | tf_op jit(solution)/shard_map/all_to_all | solution.py:204
  340.6 4.2 copy-start.6
  346.3 14.6 %copy-start.9 = (f32[2,8,128,128]{3,1,2,0:T(8,128)S(1)}, f32[2,8,128,128]{3,1,2,0:T(8,128)}, u32[]{:S(2)}) copy-start(f32[2,8,128,128]{3,1,2,0:T(8,128)} %get-tuple-element.81) | copy-start | bytes 3145732
  356.3 4.8 copy-start.1
  389.3 4.4 copy-start.5
  395.3 12.0 %copy-start.3 = (f32[128,2048]{1,0:T(8,128)S(1)}, f32[128,2048]{1,0:T(8,128)}, u32[]{:S(2)}) copy-start(f32[128,2048]{1,0:T(8,128)} %get-tuple-element.69) | copy-start | bytes 3145732
  395.3 12.9 %copy-start.4 = (f32[128,2048]{1,0:T(8,128)S(1)}, f32[128,2048]{1,0:T(8,128)}, u32[]{:S(2)}) copy-start(f32[128,2048]{1,0:T(8,128)} %get-tuple-element.68) | copy-start | bytes 3145732
  403.8 11.0 %copy-start.2 = (f32[128,2048]{1,0:T(8,128)S(1)}, f32[128,2048]{1,0:T(8,128)}, u32[]{:S(2)}) copy-start(f32[128,2048]{1,0:T(8,128)} %copy-done.1) | copy-start | bytes 3145732
  403.8 11.0 %copy-start.7 = (f32[128,2048]{1,0:T(8,128)S(1)}, f32[128,2048]{1,0:T(8,128)}, u32[]{:S(2)}) copy-start(f32[128,2048]{1,0:T(8,128)} %convolution_add_fusion.12) | copy-start | bytes 3145732
  403.8 11.0 %copy-start.8 = (f32[128,2048]{1,0:T(8,128)S(1)}, f32[128,2048]{1,0:T(8,128)}, u32[]{:S(2)}) copy-start(f32[128,2048]{1,0:T(8,128)} %fusion.195) | copy-start | bytes 3145732
  444.1 60.6 %copy-start.10 = (bf16[128,2048]{1,0:T(8,128)(2,1)S(1)}, bf16[128,2048]{1,0:T(8,128)(2,1)}, u32[]{:S(2)}) copy-start(bf16[128,2048]{1,0:T(8,128)(2,1)} %param.15) | copy-start | bytes 1572868
  451.9 47.0 %all-to-all-start.4 = ((f32[2,16,16384]{2,0,1:T(2,128)}), f32[2,16,16384]{2,0,1:T(2,128)S(1)}, u32[]{:S(2)}, u32[]{:S(2)}) async-start(f32[2,16,16384]{2,0,1:T(2,128)} %copy.179), calls=%async_computation.4 | async-start | bytes 4194304 | tf_op jit(solution)/shard_map/all_to_all | solution.py:216
  457.9 184.8 %all-reduce.2.cloned.1.call-start = ((), (), s32[]{:S(2)}) async-start(), calls=%async_computation.6 | async-start | bytes 2097152 | tf_op jit(solution)/shard_map/psum | solution.py:237
  459.1 9.5 %collective-permute-start.18 = (bf16[127,2048]{1,0:T(8,128)(2,1)S(1)}, bf16[127,2048]{1,0:T(8,128)(2,1)S(1)}, u32[]{:S(2)}, u32[]{:S(2)}) collective-permute-start(bf16[127,2048]{1,0:T(8,128)(2,1)S(1)} %slice.29), channel_id=1, source_target_pairs={{0,2},{2,4},{4,6},{6,8},{8,10},{10,12},{12,14},{14,16},{16,18},{18... | collective-permute-start | bytes 1560584 | tf_op jit(solution)/shard_map/ppermute | solution.py:33
  462.2 4.4 collective-permute-start.17
  507.2 24.6 %collective-permute-start.15 = (bf16[127,2048]{1,0:T(8,128)(2,1)}, bf16[127,2048]{1,0:T(8,128)(2,1)S(1)}, u32[]{:S(2)}, u32[]{:S(2)}) collective-permute-start(bf16[127,2048]{1,0:T(8,128)(2,1)} %bitcast.330), channel_id=1, source_target_pairs={{2,0},{4,2},{6,4},{8,6},{10,8},{12,10},{14,12},{16,14},{18,16},{20... | collective-permute-start | bytes 1560584 | tf_op jit(solution)/shard_map/ppermute | solution.py:33
  532.9 16.6 %copy-start.11 = (bf16[1,134,2048]{2,1,0:T(8,128)(2,1)S(1)}, bf16[1,134,2048]{2,1,0:T(8,128)(2,1)}, u32[]{:S(2)}) copy-start(bf16[1,134,2048]{2,1,0:T(8,128)(2,1)} %maximum_bitcast_fusion.3) | copy-start | bytes 1646596
  547.8 97.9 %copy-start.13 = (bf16[7,2048]{1,0:T(8,128)(2,1)S(1)}, bf16[7,2048]{1,0:T(8,128)(2,1)}, u32[]{:S(2)}) copy-start(bf16[7,2048]{1,0:T(8,128)(2,1)} %param.20) | copy-start | bytes 86020
  547.8 97.9 %copy-start.14 = (pred[8,17]{0,1:T(8,128)(4,1)S(1)}, pred[8,17]{0,1:T(8,128)(4,1)}, u32[]{:S(2)}) copy-start(pred[8,17]{0,1:T(8,128)(4,1)} %constant.228) | copy-start | bytes 412
  548.2 96.7 %collective-permute-start.16 = (bf16[6,2048]{1,0:T(8,128)(2,1)S(1)}, bf16[6,2048]{1,0:T(8,128)(2,1)S(1)}, u32[]{:S(2)}, u32[]{:S(2)}) collective-permute-start(bf16[6,2048]{1,0:T(8,128)(2,1)S(1)} %bitcast.394), channel_id=1, source_target_pairs={{2,0},{4,2},{6,4},{8,6},{10,8},{12,10},{14,12},{16,14},{18,16},{20... | collective-permute-start | bytes 73736 | tf_op jit(solution)/shard_map/ppermute | solution.py:33
Sparse Core Ops, SparseCore 0:
  100.5 19.4 all-gather.1
  530.6 112.0 all-reduce.1
